TPU v7x, 32 devices: a whole 2x2x4 slice. The times are simulated.
32 devices in a mesh: row: 8 (over y, x, core), col: 4 (over z).
Axes of the slice: x: 2, y: 2, z: 4, core: 2. Of those that a mesh axis runs over, the one named last changes fastest.
Arguments:
- query: bfloat16 [8, 512, 4096], P(None, 'col'), may hold values from -7 to 7
- key: bfloat16 [4096, 512], P(('row', 'col')), may hold values from -7 to 7
- value: bfloat16 [4096, 512], P(('row', 'col')), may hold values from -4 to 4
- span_order: int32 [32], replicated, may hold values from 0 to 31, each once
Outputs:
- attention: bfloat16 [4096, 4096], P(('row', 'col'))
Inputs may be any that keep to these rules, and one draw needn't show every extreme that they name: span_order is a permutation of 0 to 31.
All inputs are finite; a program needn't handle non-finite values.
Results may differ from a plain program's by a relative error of at most 0.0085.
Values may be sent and summed in bfloat16 or wider, within the bound.
No kernel may reach another device: no remote copies, remote signals or barrier semaphores. Data moves between devices by JAX's collectives and lax.ppermute only.
A program may use at most 192 MiB of HBM per device.

v0:
```python
import jax
import jax.numpy as jnp
from jax import lax
from jax.sharding import PartitionSpec as P

HEAD_DIM = 128
QHEADS = 32
KVHEADS = 4


masked_score = -1e30


def passed_along(value, axis, steps):
    count = lax.axis_size(axis)
    pairs = [(source, (source + steps) % count) for source in range(count)]
    return lax.ppermute(value, axis, pairs)


def lookup(table, indices):
    columns = jnp.arange(table.shape[0], dtype=jnp.int32)
    chosen = jnp.where(indices[:, None] == columns[None, :], table[None, :], 0)
    return jnp.sum(chosen, axis=1)


def attend(state, queries, query_places, keys, values, key_places):
    best, total, summed = state
    scores = jnp.einsum(
        "nkgd,skd->nkgs", queries, keys, preferred_element_type=jnp.float32
    ) * queries.shape[-1] ** (-0.5)
    visible = key_places[None, None, None, :] <= query_places[:, None, None, None]
    scores = jnp.where(visible, scores, masked_score)
    newest = jnp.maximum(best, jnp.max(scores, axis=-1))
    shrink = jnp.exp(best - newest)
    raised = jnp.exp(scores - newest[..., None])
    total = jnp.sum(raised, axis=-1)
    weights = raised.astype(jnp.bfloat16)
    update = jnp.einsum("nkgs,skd->nkgd", weights, values, preferred_element_type=jnp.float32)
    summed = update
    return (newest, total, summed)


def finish(state):
    best, total, summed = state
    floor = jnp.maximum(total, 1.0)
    return ((summed / floor[..., None]).astype(jnp.bfloat16), best + jnp.log(floor))


def combine(partials, log_sums):
    highest = jnp.max(log_sums, axis=0)
    combined = highest + jnp.log(jnp.sum(jnp.exp(log_sums - highest), axis=0))
    scale_each = jnp.exp(log_sums - combined)
    return jnp.sum(scale_each[..., None] * partials.astype(jnp.float32), axis=0)


def empty_state(lead):
    best = jnp.full(lead, masked_score, jnp.float32)
    total = jnp.zeros(lead, jnp.float32)
    summed = jnp.zeros(lead + (HEAD_DIM,), jnp.float32)
    return (best, total, summed)


def shards(query, key, value, span_order):
    rows = lax.axis_size("row")
    columns = lax.axis_size("col")
    row_id = lax.axis_index("row")
    col_id = lax.axis_index("col")
    block_rows = key.shape[0]
    group = QHEADS // KVHEADS
    offsets = jnp.arange(block_rows, dtype=jnp.int32)
    tile_spans = jnp.arange(rows, dtype=jnp.int32) * columns + col_id
    tile_orders = lookup(span_order, tile_spans)
    tile_places = tile_orders[:, None] * block_rows + offsets[None, :]
    block_orders = lookup(span_order, row_id * columns + jnp.arange(columns, dtype=jnp.int32))
    block_places = block_orders[:, None] * block_rows + offsets[None, :]
    outputs = []
    for head in range(KVHEADS):
        low = head * group * HEAD_DIM
        high = (head + 1) * group * HEAD_DIM
        head_queries = query[:, :, low:high].reshape(rows, block_rows, 1, group, HEAD_DIM)
        head_keys = key[:, head * HEAD_DIM : (head + 1) * HEAD_DIM]
        head_values = value[:, head * HEAD_DIM : (head + 1) * HEAD_DIM]
        pair = jnp.stack([head_keys, head_values]).reshape(2, block_rows, 1, HEAD_DIM)
        held = jnp.zeros((columns,) + pair.shape, pair.dtype)

        def turn(step, carry):
            stored, moving = carry
            source = (col_id - step) % columns
            stored = lax.dynamic_update_index_in_dim(stored, moving, source, 0)
            moving = passed_along(moving, "col", 1)
            return (stored, moving)

        held, pair = lax.fori_loop(0, columns - 1, turn, (held, pair))
        held = lax.dynamic_update_index_in_dim(held, pair, (col_id - (columns - 1)) % columns, 0)

        def tile_step(unused, inputs, held=held):
            tile_queries, tile_spots, tile_order = inputs
            start_state = empty_state((block_rows, 1, group))
            all_keys = held[:, 0].reshape(columns * block_rows, 1, HEAD_DIM)
            all_values = held[:, 1].reshape(columns * block_rows, 1, HEAD_DIM)
            state = attend(
                start_state,
                tile_queries,
                tile_spots,
                all_keys,
                all_values,
                block_places.reshape(columns * block_rows),
            )
            return (unused, finish(state))

        unused, results = lax.scan(
            tile_step, jnp.int32(0), (head_queries, tile_places, tile_orders)
        )
        partial_value, log_sum = results
        partial_value = lax.all_to_all(
            partial_value.reshape(rows, block_rows, group * HEAD_DIM),
            "row",
            split_axis=0,
            concat_axis=0,
            tiled=True,
        )
        log_sum = lax.all_to_all(
            log_sum.reshape(rows, block_rows, group), "row", split_axis=0, concat_axis=0, tiled=True
        )
        merged = combine(
            partial_value.reshape(rows, block_rows, 1, group, HEAD_DIM),
            log_sum.reshape(rows, block_rows, 1, group),
        )
        outputs.append(merged.reshape(block_rows, group * HEAD_DIM))
    return jnp.concatenate(outputs, axis=1).astype(jnp.bfloat16)


def solution(mesh):
    placed = (P(None, "col", None), P(("row", "col"), None), P(("row", "col"), None), P())
    return jax.shard_map(
        shards, mesh=mesh, in_specs=placed, out_specs=P(("row", "col"), None), check_vma=False
    )
```

profile of v0, /device:TPU:0, one launch (start us, length us, event | category | flops | bytes accessed | tf_op | source)
XLA Modules:
  0.0 369.5 jit_solution(8904010601652355132)
XLA Ops:
  11.8 19.5 %while.120 = (s32[]{:T(128)}, bf16[4,2,128,1,128]{4,2,0,3,1:T(8,128)(2,1)S(1)}, bf16[2,128,1,128]{3,1,0,2:T(8,128)(2,1)S(1)}, s32[]{:T(128)}, s32[]{:T(128)}, /*index=5*/s32[]{:T(128)}, s32[]{:T(128)}, s32[]{:T(128)}) while((s32[]{:T(128)}, bf16[4,2,128,1,128]{4,2,0,3,1:T(8,128)(2,1)S(1)}, bf16[2,128,1,128]{3,1,0,2:T(8,128)(2,1)S(1)}, ...), condition=%wide.region_2.3_spmd, body=%wide.region_1.2_spmd.sunk | while | flops 17 | bytes 524572 | solution.py:93
  19.2 6.0 %collective-permute-done = bf16[2,128,1,128]{3,1,0,2:T(8,128)(2,1)S(1)} collective-permute-done((bf16[2,128,1,128]{3,1,0,2:T(8,128)(2,1)S(1)}, bf16[2,128,1,128]{3,1,0,2:T(8,128)(2,1)S(1)}, u32[]{:S(2)}, u32[]{:S(2)}) %collective-permute-start) | collective-permute-done | bytes 65568 | tf_op jit(solution)/shard_map/while/body/eval_jaxpr/ppermute | solution.py:17
  25.3 6.0 %collective-permute-done = bf16[2,128,1,128]{3,1,0,2:T(8,128)(2,1)S(1)} collective-permute-done((bf16[2,128,1,128]{3,1,0,2:T(8,128)(2,1)S(1)}, bf16[2,128,1,128]{3,1,0,2:T(8,128)(2,1)S(1)}, u32[]{:S(2)}, u32[]{:S(2)}) %collective-permute-start) | collective-permute-done | bytes 65568 | tf_op jit(solution)/shard_map/while/body/eval_jaxpr/ppermute | solution.py:17
  32.4 31.1 %while.124 = (s32[]{:T(128)}, bf16[8,128,1,8,128]{1,4,3,0,2:T(8,128)(2,1)S(1)}, f32[8,128,1,8]{1,3,2,0:T(8,128)}, s32[8,128]{1,0:T(8,128)S(1)}, bf16[8,128,1,8,1...) while((s32[]{:T(128)}, ...), condition=%wide.region_7.8_spmd.clone, body=%wide.region_4.7_spmd.clone.sunk | while | flops 272436736 | bytes 8837741 | solution.py:111
  71.5 18.5 %while.121 = (s32[]{:T(128)}, bf16[4,2,128,1,128]{4,2,0,3,1:T(8,128)(2,1)S(1)}, bf16[2,128,1,128]{3,1,0,2:T(8,128)(2,1)S(1)}, s32[]{:T(128)}, s32[]{:T(128)}, /*index=5*/s32[]{:T(128)}, s32[]{:T(128)}, s32[]{:T(128)}) while((s32[]{:T(128)}, bf16[4,2,128,1,128]{4,2,0,3,1:T(8,128)(2,1)S(1)}, bf16[2,128,1,128]{3,1,0,2:T(8,128)(2,1)S(1)}, ...), condition=%wide.region_12.13_spmd, body=%wide.region_11.12_spmd.sunk | while | flops 17 | bytes 524572 | solution.py:93
  71.6 6.2 %collective-permute-done.1 = bf16[2,128,1,128]{3,1,0,2:T(8,128)(2,1)S(1)} collective-permute-done((bf16[2,128,1,128]{3,1,0,2:T(8,128)(2,1)S(1)}, bf16[2,128,1,128]{3,1,0,2:T(8,128)(2,1)S(1)}, u32[]{:S(2)}, u32[]{:S(2)}) %collective-permute-start.1) | collective-permute-done | bytes 65568 | tf_op jit(solution)/shard_map/while/body/eval_jaxpr/ppermute | solution.py:17
  77.9 6.0 %collective-permute-done.1 = bf16[2,128,1,128]{3,1,0,2:T(8,128)(2,1)S(1)} collective-permute-done((bf16[2,128,1,128]{3,1,0,2:T(8,128)(2,1)S(1)}, bf16[2,128,1,128]{3,1,0,2:T(8,128)(2,1)S(1)}, u32[]{:S(2)}, u32[]{:S(2)}) %collective-permute-start.1) | collective-permute-done | bytes 65568 | tf_op jit(solution)/shard_map/while/body/eval_jaxpr/ppermute | solution.py:17
  84.0 6.0 %collective-permute-done.1 = bf16[2,128,1,128]{3,1,0,2:T(8,128)(2,1)S(1)} collective-permute-done((bf16[2,128,1,128]{3,1,0,2:T(8,128)(2,1)S(1)}, bf16[2,128,1,128]{3,1,0,2:T(8,128)(2,1)S(1)}, u32[]{:S(2)}, u32[]{:S(2)}) %collective-permute-start.1) | collective-permute-done | bytes 65568 | tf_op jit(solution)/shard_map/while/body/eval_jaxpr/ppermute | solution.py:17
  91.1 31.1 %while.125 = (s32[]{:T(128)}, bf16[8,128,1,8,128]{1,4,3,0,2:T(8,128)(2,1)S(1)}, f32[8,128,1,8]{1,3,2,0:T(8,128)}, s32[8,128]{1,0:T(8,128)S(1)}, bf16[8,128,1,8,1...) while((s32[]{:T(128)}, ...), condition=%wide.region_16.17_spmd.clone, body=%wide.region_13.16_spmd.clone.sunk | while | flops 272436736 | bytes 8837741 | solution.py:111
  126.7 18.8 %while.122 = (s32[]{:T(128)}, bf16[4,2,128,1,128]{4,2,0,3,1:T(8,128)(2,1)S(1)}, bf16[2,128,1,128]{3,1,0,2:T(8,128)(2,1)S(1)}, s32[]{:T(128)}, s32[]{:T(128)}, /*index=5*/s32[]{:T(128)}, s32[]{:T(128)}, s32[]{:T(128)}) while((s32[]{:T(128)}, bf16[4,2,128,1,128]{4,2,0,3,1:T(8,128)(2,1)S(1)}, bf16[2,128,1,128]{3,1,0,2:T(8,128)(2,1)S(1)}, ...), condition=%wide.region_21.22_spmd, body=%wide.region_20.21_spmd.sunk | while | flops 17 | bytes 524572 | solution.py:93
  126.8 6.0 %collective-permute-done.2 = bf16[2,128,1,128]{3,1,0,2:T(8,128)(2,1)S(1)} collective-permute-done((bf16[2,128,1,128]{3,1,0,2:T(8,128)(2,1)S(1)}, bf16[2,128,1,128]{3,1,0,2:T(8,128)(2,1)S(1)}, u32[]{:S(2)}, u32[]{:S(2)}) %collective-permute-start.2) | collective-permute-done | bytes 65568 | tf_op jit(solution)/shard_map/while/body/eval_jaxpr/ppermute | solution.py:17
  132.9 6.6 %collective-permute-done.2 = bf16[2,128,1,128]{3,1,0,2:T(8,128)(2,1)S(1)} collective-permute-done((bf16[2,128,1,128]{3,1,0,2:T(8,128)(2,1)S(1)}, bf16[2,128,1,128]{3,1,0,2:T(8,128)(2,1)S(1)}, u32[]{:S(2)}, u32[]{:S(2)}) %collective-permute-start.2) | collective-permute-done | bytes 65568 | tf_op jit(solution)/shard_map/while/body/eval_jaxpr/ppermute | solution.py:17
  139.6 6.0 %collective-permute-done.2 = bf16[2,128,1,128]{3,1,0,2:T(8,128)(2,1)S(1)} collective-permute-done((bf16[2,128,1,128]{3,1,0,2:T(8,128)(2,1)S(1)}, bf16[2,128,1,128]{3,1,0,2:T(8,128)(2,1)S(1)}, u32[]{:S(2)}, u32[]{:S(2)}) %collective-permute-start.2) | collective-permute-done | bytes 65568 | tf_op jit(solution)/shard_map/while/body/eval_jaxpr/ppermute | solution.py:17
  146.7 31.2 %while.126 = (s32[]{:T(128)}, bf16[8,128,1,8,128]{1,4,3,0,2:T(8,128)(2,1)S(1)}, f32[8,128,1,8]{1,3,2,0:T(8,128)}, s32[8,128]{1,0:T(8,128)S(1)}, bf16[8,128,1,8,1...) while((s32[]{:T(128)}, ...), condition=%wide.region_25.26_spmd.clone, body=%wide.region_22.25_spmd.clone.sunk | while | flops 272436736 | bytes 8837741 | solution.py:111
  181.6 18.5 %while.123 = (s32[]{:T(128)}, bf16[4,2,128,1,128]{4,2,0,3,1:T(8,128)(2,1)S(1)}, bf16[2,128,1,128]{3,1,0,2:T(8,128)(2,1)S(1)}, s32[]{:T(128)}, s32[]{:T(128)}, /*index=5*/s32[]{:T(128)}, s32[]{:T(128)}, s32[]{:T(128)}) while((s32[]{:T(128)}, bf16[4,2,128,1,128]{4,2,0,3,1:T(8,128)(2,1)S(1)}, bf16[2,128,1,128]{3,1,0,2:T(8,128)(2,1)S(1)}, ...), condition=%wide.region_30.31_spmd, body=%wide.region_29.30_spmd.sunk | while | flops 17 | bytes 524572 | solution.py:93
  181.7 6.2 %collective-permute-done.3 = bf16[2,128,1,128]{3,1,0,2:T(8,128)(2,1)S(1)} collective-permute-done((bf16[2,128,1,128]{3,1,0,2:T(8,128)(2,1)S(1)}, bf16[2,128,1,128]{3,1,0,2:T(8,128)(2,1)S(1)}, u32[]{:S(2)}, u32[]{:S(2)}) %collective-permute-start.3) | collective-permute-done | bytes 65568 | tf_op jit(solution)/shard_map/while/body/eval_jaxpr/ppermute | solution.py:17
  188.0 6.0 %collective-permute-done.3 = bf16[2,128,1,128]{3,1,0,2:T(8,128)(2,1)S(1)} collective-permute-done((bf16[2,128,1,128]{3,1,0,2:T(8,128)(2,1)S(1)}, bf16[2,128,1,128]{3,1,0,2:T(8,128)(2,1)S(1)}, u32[]{:S(2)}, u32[]{:S(2)}) %collective-permute-start.3) | collective-permute-done | bytes 65568 | tf_op jit(solution)/shard_map/while/body/eval_jaxpr/ppermute | solution.py:17
  194.1 6.0 %collective-permute-done.3 = bf16[2,128,1,128]{3,1,0,2:T(8,128)(2,1)S(1)} collective-permute-done((bf16[2,128,1,128]{3,1,0,2:T(8,128)(2,1)S(1)}, bf16[2,128,1,128]{3,1,0,2:T(8,128)(2,1)S(1)}, u32[]{:S(2)}, u32[]{:S(2)}) %collective-permute-start.3) | collective-permute-done | bytes 65568 | tf_op jit(solution)/shard_map/while/body/eval_jaxpr/ppermute | solution.py:17
  208.5 26.6 %while.127 = (s32[]{:T(128)}, bf16[8,128,1,8,128]{1,4,3,0,2:T(8,128)(2,1)S(1)}, f32[8,128,1,8]{1,3,2,0:T(8,128)S(1)}, s32[8,128]{1,0:T(8,128)S(1)}, bf16[8,128,1...) while((s32[]{:T(128)}, ...), condition=%wide.region_34.35_spmd.clone, body=%wide.region_31.34_spmd.clone.sunk | while | flops 272436736 | bytes 8837233 | solution.py:111
  235.2 9.0 %all_to_all.40 = f32[8,128,8]{1,2,0:T(8,128)S(1)} all-to-all(f32[8,128,8]{1,2,0:T(8,128)S(1)} %bitcast.360), channel_id=1, replica_groups=mesh['row'=8,'col'=4] {'row'}, dimensions={0} | all-to-all | bytes 65536 | tf_op jit(solution)/shard_map/all_to_all | solution.py:122
  244.2 30.2 %all_to_all.41 = bf16[8,128,1024]{1,2,0:T(8,128)(2,1)S(1)} all-to-all(bf16[8,128,1024]{1,2,0:T(8,128)(2,1)} %bitcast.349), channel_id=1, replica_groups=mesh['row'=8,'col'=4] {'row'}, dimensions={0} | all-to-all | bytes 4194304 | tf_op jit(solution)/shard_map/all_to_all | solution.py:115
  274.4 29.7 %all_to_all.42 = bf16[8,128,1024]{1,2,0:T(8,128)(2,1)} all-to-all(bf16[8,128,1024]{1,2,0:T(8,128)(2,1)S(1)} %bitcast.350), channel_id=1, replica_groups=mesh['row'=8,'col'=4] {'row'}, dimensions={0} | all-to-all | bytes 4194304 | tf_op jit(solution)/shard_map/all_to_all | solution.py:115
  308.6 26.5 %all-to-all-done.5 = bf16[8,128,1024]{1,2,0:T(8,128)(2,1)} async-done(((bf16[8,128,1024]{1,2,0:T(8,128)(2,1)}), bf16[8,128,1024]{1,2,0:T(8,128)(2,1)}, u32[]{:S(2)}, u32[]{:S(2)}) %all-to-all-start.5) | async-done | bytes 2097184 | tf_op jit(solution)/shard_map/all_to_all | solution.py:115
  343.5 22.6 %all-to-all-done.7 = bf16[8,128,1024]{1,2,0:T(8,128)(2,1)} async-done(((bf16[8,128,1024]{1,2,0:T(8,128)(2,1)}), bf16[8,128,1024]{1,2,0:T(8,128)(2,1)}, u32[]{:S(2)}, u32[]{:S(2)}) %all-to-all-start.7) | async-done | bytes 2097184 | tf_op jit(solution)/shard_map/all_to_all | solution.py:115
  (495 shorter events, 181.6 us)
Async XLA Ops:
  11.8 7.4 %collective-permute-start = (bf16[2,128,1,128]{3,1,0,2:T(8,128)(2,1)S(1)}, bf16[2,128,1,128]{3,1,0,2:T(8,128)(2,1)S(1)}, u32[]{:S(2)}, u32[]{:S(2)}) collective-permute-start(bf16[2,128,1,128]{3,1,0,2:T(8,128)(2,1)S(1)} %copy.169), channel_id=1, source_target_pairs={{0,1},{1,2},{2,3},{3,0},{4,5},{5,6},{6,7},{7,4},{8,9},{9,10},{10,1... | collective-permute-start | bytes 196616 | tf_op jit(solution)/shard_map/while/body/eval_jaxpr/ppermute | solution.py:17
  19.2 6.1 %collective-permute-start = (bf16[2,128,1,128]{3,1,0,2:T(8,128)(2,1)S(1)}, bf16[2,128,1,128]{3,1,0,2:T(8,128)(2,1)S(1)}, u32[]{:S(2)}, u32[]{:S(2)}) collective-permute-start(bf16[2,128,1,128]{3,1,0,2:T(8,128)(2,1)S(1)} %copy.169), channel_id=1, source_target_pairs={{0,1},{1,2},{2,3},{3,0},{4,5},{5,6},{6,7},{7,4},{8,9},{9,10},{10,1... | collective-permute-start | bytes 196616 | tf_op jit(solution)/shard_map/while/body/eval_jaxpr/ppermute | solution.py:17
  25.2 6.1 %collective-permute-start = (bf16[2,128,1,128]{3,1,0,2:T(8,128)(2,1)S(1)}, bf16[2,128,1,128]{3,1,0,2:T(8,128)(2,1)S(1)}, u32[]{:S(2)}, u32[]{:S(2)}) collective-permute-start(bf16[2,128,1,128]{3,1,0,2:T(8,128)(2,1)S(1)} %copy.169), channel_id=1, source_target_pairs={{0,1},{1,2},{2,3},{3,0},{4,5},{5,6},{6,7},{7,4},{8,9},{9,10},{10,1... | collective-permute-start | bytes 196616 | tf_op jit(solution)/shard_map/while/body/eval_jaxpr/ppermute | solution.py:17
  63.6 7.9 %copy-start.2 = (bf16[8,128,1,8,128]{1,4,3,0,2:T(8,128)(2,1)}, bf16[8,128,1,8,128]{1,4,3,0,2:T(8,128)(2,1)S(1)}, u32[]{:S(2)}) copy-start(bf16[8,128,1,8,128]{1,4,3,0,2:T(8,128)(2,1)S(1)} %get-tuple-element.608) | copy-start | bytes 6291460
  63.6 114.3 %all-to-all-start = ((f32[8,128,8]{1,2,0:T(8,128)}), f32[8,128,8]{1,2,0:T(8,128)S(1)}, u32[]{:S(2)}, u32[]{:S(2)}) async-start(f32[8,128,8]{1,2,0:T(8,128)} %bitcast.9), calls=%async_computation | async-start | bytes 65536 | tf_op jit(solution)/shard_map/all_to_all | solution.py:122
  71.5 6.3 %collective-permute-start.1 = (bf16[2,128,1,128]{3,1,0,2:T(8,128)(2,1)S(1)}, bf16[2,128,1,128]{3,1,0,2:T(8,128)(2,1)S(1)}, u32[]{:S(2)}, u32[]{:S(2)}) collective-permute-start(bf16[2,128,1,128]{3,1,0,2:T(8,128)(2,1)S(1)} %copy.150), channel_id=1, source_target_pairs={{0,1},{1,2},{2,3},{3,0},{4,5},{5,6},{6,7},{7,4},{8,9},{9,10},{10,1... | collective-permute-start | bytes 196616 | tf_op jit(solution)/shard_map/while/body/eval_jaxpr/ppermute | solution.py:17
  77.8 6.1 %collective-permute-start.1 = (bf16[2,128,1,128]{3,1,0,2:T(8,128)(2,1)S(1)}, bf16[2,128,1,128]{3,1,0,2:T(8,128)(2,1)S(1)}, u32[]{:S(2)}, u32[]{:S(2)}) collective-permute-start(bf16[2,128,1,128]{3,1,0,2:T(8,128)(2,1)S(1)} %copy.150), channel_id=1, source_target_pairs={{0,1},{1,2},{2,3},{3,0},{4,5},{5,6},{6,7},{7,4},{8,9},{9,10},{10,1... | collective-permute-start | bytes 196616 | tf_op jit(solution)/shard_map/while/body/eval_jaxpr/ppermute | solution.py:17
  83.9 6.1 %collective-permute-start.1 = (bf16[2,128,1,128]{3,1,0,2:T(8,128)(2,1)S(1)}, bf16[2,128,1,128]{3,1,0,2:T(8,128)(2,1)S(1)}, u32[]{:S(2)}, u32[]{:S(2)}) collective-permute-start(bf16[2,128,1,128]{3,1,0,2:T(8,128)(2,1)S(1)} %copy.150), channel_id=1, source_target_pairs={{0,1},{1,2},{2,3},{3,0},{4,5},{5,6},{6,7},{7,4},{8,9},{9,10},{10,1... | collective-permute-start | bytes 196616 | tf_op jit(solution)/shard_map/while/body/eval_jaxpr/ppermute | solution.py:17
  122.2 4.4 %copy-start.3 = (bf16[8,128,1,8,128]{1,4,3,0,2:T(8,128)(2,1)}, bf16[8,128,1,8,128]{1,4,3,0,2:T(8,128)(2,1)S(1)}, u32[]{:S(2)}) copy-start(bf16[8,128,1,8,128]{1,4,3,0,2:T(8,128)(2,1)S(1)} %get-tuple-element.612) | copy-start | bytes 6291460
  126.7 6.1 %collective-permute-start.2 = (bf16[2,128,1,128]{3,1,0,2:T(8,128)(2,1)S(1)}, bf16[2,128,1,128]{3,1,0,2:T(8,128)(2,1)S(1)}, u32[]{:S(2)}, u32[]{:S(2)}) collective-permute-start(bf16[2,128,1,128]{3,1,0,2:T(8,128)(2,1)S(1)} %copy.131), channel_id=1, source_target_pairs={{0,1},{1,2},{2,3},{3,0},{4,5},{5,6},{6,7},{7,4},{8,9},{9,10},{10,1... | collective-permute-start | bytes 196616 | tf_op jit(solution)/shard_map/while/body/eval_jaxpr/ppermute | solution.py:17
  132.9 6.6 %collective-permute-start.2 = (bf16[2,128,1,128]{3,1,0,2:T(8,128)(2,1)S(1)}, bf16[2,128,1,128]{3,1,0,2:T(8,128)(2,1)S(1)}, u32[]{:S(2)}, u32[]{:S(2)}) collective-permute-start(bf16[2,128,1,128]{3,1,0,2:T(8,128)(2,1)S(1)} %copy.131), channel_id=1, source_target_pairs={{0,1},{1,2},{2,3},{3,0},{4,5},{5,6},{6,7},{7,4},{8,9},{9,10},{10,1... | collective-permute-start | bytes 196616 | tf_op jit(solution)/shard_map/while/body/eval_jaxpr/ppermute | solution.py:17
  139.5 6.1 %collective-permute-start.2 = (bf16[2,128,1,128]{3,1,0,2:T(8,128)(2,1)S(1)}, bf16[2,128,1,128]{3,1,0,2:T(8,128)(2,1)S(1)}, u32[]{:S(2)}, u32[]{:S(2)}) collective-permute-start(bf16[2,128,1,128]{3,1,0,2:T(8,128)(2,1)S(1)} %copy.131), channel_id=1, source_target_pairs={{0,1},{1,2},{2,3},{3,0},{4,5},{5,6},{6,7},{7,4},{8,9},{9,10},{10,1... | collective-permute-start | bytes 196616 | tf_op jit(solution)/shard_map/while/body/eval_jaxpr/ppermute | solution.py:17
  177.9 26.1 %copy-start.5 = (bf16[8,128,1,8,128]{1,4,3,0,2:T(8,128)(2,1)}, bf16[8,128,1,8,128]{1,4,3,0,2:T(8,128)(2,1)S(1)}, u32[]{:S(2)}) copy-start(bf16[8,128,1,8,128]{1,4,3,0,2:T(8,128)(2,1)S(1)} %get-tuple-element.616) | copy-start | bytes 6291460
  177.9 26.1 %all-to-all-start.2 = ((f32[8,128,8]{1,2,0:T(8,128)}), f32[8,128,8]{1,2,0:T(8,128)S(1)}, u32[]{:S(2)}, u32[]{:S(2)}) async-start(f32[8,128,8]{1,2,0:T(8,128)} %bitcast.17), calls=%async_computation.2 | async-start | bytes 65536 | tf_op jit(solution)/shard_map/all_to_all | solution.py:122
  181.6 6.4 %collective-permute-start.3 = (bf16[2,128,1,128]{3,1,0,2:T(8,128)(2,1)S(1)}, bf16[2,128,1,128]{3,1,0,2:T(8,128)(2,1)S(1)}, u32[]{:S(2)}, u32[]{:S(2)}) collective-permute-start(bf16[2,128,1,128]{3,1,0,2:T(8,128)(2,1)S(1)} %copy.112), channel_id=1, source_target_pairs={{0,1},{1,2},{2,3},{3,0},{4,5},{5,6},{6,7},{7,4},{8,9},{9,10},{10,1... | collective-permute-start | bytes 196616 | tf_op jit(solution)/shard_map/while/body/eval_jaxpr/ppermute | solution.py:17
  188.0 6.1 %collective-permute-start.3 = (bf16[2,128,1,128]{3,1,0,2:T(8,128)(2,1)S(1)}, bf16[2,128,1,128]{3,1,0,2:T(8,128)(2,1)S(1)}, u32[]{:S(2)}, u32[]{:S(2)}) collective-permute-start(bf16[2,128,1,128]{3,1,0,2:T(8,128)(2,1)S(1)} %copy.112), channel_id=1, source_target_pairs={{0,1},{1,2},{2,3},{3,0},{4,5},{5,6},{6,7},{7,4},{8,9},{9,10},{10,1... | collective-permute-start | bytes 196616 | tf_op jit(solution)/shard_map/while/body/eval_jaxpr/ppermute | solution.py:17
  194.0 6.1 %collective-permute-start.3 = (bf16[2,128,1,128]{3,1,0,2:T(8,128)(2,1)S(1)}, bf16[2,128,1,128]{3,1,0,2:T(8,128)(2,1)S(1)}, u32[]{:S(2)}, u32[]{:S(2)}) collective-permute-start(bf16[2,128,1,128]{3,1,0,2:T(8,128)(2,1)S(1)} %copy.112), channel_id=1, source_target_pairs={{0,1},{1,2},{2,3},{3,0},{4,5},{5,6},{6,7},{7,4},{8,9},{9,10},{10,1... | collective-permute-start | bytes 196616 | tf_op jit(solution)/shard_map/while/body/eval_jaxpr/ppermute | solution.py:17
  204.0 31.1 %all-to-all-start.4 = ((f32[8,128,8]{1,2,0:T(8,128)}), f32[8,128,8]{1,2,0:T(8,128)S(1)}, u32[]{:S(2)}, u32[]{:S(2)}) async-start(f32[8,128,8]{1,2,0:T(8,128)} %bitcast.25), calls=%async_computation.4 | async-start | bytes 65536 | tf_op jit(solution)/shard_map/all_to_all | solution.py:122
  235.1 9.0 %copy-start.1 = (bf16[8,128,1,8,128]{1,4,3,0,2:T(8,128)(2,1)}, bf16[8,128,1,8,128]{1,4,3,0,2:T(8,128)(2,1)S(1)}, u32[]{:S(2)}) copy-start(bf16[8,128,1,8,128]{1,4,3,0,2:T(8,128)(2,1)S(1)} %get-tuple-element.620) | copy-start | bytes 6291460
  244.2 30.2 %copy-start.4 = (bf16[8,128,1,8,128]{1,4,3,0,2:T(8,128)(2,1)S(1)}, bf16[8,128,1,8,128]{1,4,3,0,2:T(8,128)(2,1)}, u32[]{:S(2)}) copy-start(bf16[8,128,1,8,128]{1,4,3,0,2:T(8,128)(2,1)} %copy-done.3) | copy-start | bytes 6291460
  304.1 31.0 %all-to-all-start.5 = ((bf16[8,128,1024]{1,2,0:T(8,128)(2,1)}), bf16[8,128,1024]{1,2,0:T(8,128)(2,1)}, u32[]{:S(2)}, u32[]{:S(2)}) async-start(bf16[8,128,1024]{1,2,0:T(8,128)(2,1)} %bitcast.351), calls=%async_computation.5 | async-start | bytes 4194304 | tf_op jit(solution)/shard_map/all_to_all | solution.py:115
  335.1 31.0 %all-to-all-start.7 = ((bf16[8,128,1024]{1,2,0:T(8,128)(2,1)}), bf16[8,128,1024]{1,2,0:T(8,128)(2,1)}, u32[]{:S(2)}, u32[]{:S(2)}) async-start(bf16[8,128,1024]{1,2,0:T(8,128)(2,1)} %bitcast.348), calls=%async_computation.7 | async-start | bytes 4194304 | tf_op jit(solution)/shard_map/all_to_all | solution.py:115
  339.5 1.6 copy-start
where the time goes:
time: 372 us; the launch traced here: 369 us
  waiting for transfers between devices  120 us (32%)
  blocking collectives  69 us (19%)
  matrix products  68.2 us (18%)
  other arithmetic  49 us (13%)
  local copies, waits for them, and re-layouts  36.6 us (10%)
  starting transfers between devices  23.6 us (6%)
    ppermute x12, waiting for transfers between devices, passed_along(): return lax.ppermute(value, axis, pairs)  71.3 us
    all_to_all x2, blocking collectives, shards(): lax.all_to_all(partial_value.reshape(rows, block_rows, group * HEAD_DIM),...  59.9 us
    all_to_all x2, waiting for transfers between devices, shards(): lax.all_to_all(partial_value.reshape(rows, block_rows, group * HEAD_DIM),...  49.1 us
    dot_general x32, matrix products, attend(): jnp.einsum('nkgd,skd->nkgs', queries, keys, preferred_element_type=jnp.fl...  48.9 us
    reduce_sum x32, other arithmetic, attend(): total = jnp.sum(raised, axis=-1)  21.5 us
    dot_general x32, matrix products, attend(): jnp.einsum('nkgs,skd->nkgd', weights, values, preferred_element_type=jnp....  19.3 us
    unnamed x16, local copies, waits for them, and re-layouts  15.7 us
    dynamic_update_slice x32, other arithmetic, shards(): lax.scan(tile_step, jnp.int32(0), (head_queries, tile_places, tile_orders))  14.6 us
  transfers between devices with their start and end apart: 17, of which 14 were waited for; matrix products, arithmetic and copies ran while one was open for 29% of the time, Pallas kernels for 0%

commit v1 on v0

v1 whole, which is shorter than its diff:
```python
import functools
import math

import jax
import jax.numpy as jnp
from jax import lax
from jax.experimental import pallas as pl
from jax.experimental.pallas import tpu as pltpu
from jax.sharding import PartitionSpec as P

HEAD_DIM = 128
QHEADS = 32
KVHEADS = 4
TILE_SPANS = 4

masked_score = -1e30


def attention_kernel(order, ids, query, mine, other, out, keys, values, *, spans, columns, tokens):
    step = pl.program_id(0)
    heads = query.shape[-1] // HEAD_DIM
    half = tokens // 2
    wide = heads * tokens

    @pl.when(step == 0)
    def _():
        parity = ids[2]
        first = pl.multiple_of(parity * half, half)
        second = pl.multiple_of((1 - parity) * half, half)

        def place(span, carry):
            spot = order[span]
            keys[spot, pl.ds(first, half), :] = mine[span, 0]
            keys[spot, pl.ds(second, half), :] = other[span, 0]
            low = jnp.where(parity == 0, mine[span, 1], other[span, 1])
            high = jnp.where(parity == 0, other[span, 1], mine[span, 1])
            whole = jnp.concatenate([low, high], axis=0).astype(jnp.float32)
            values[spot, :HEAD_DIM, :] = whole.T.astype(jnp.bfloat16)
            values[spot, HEAD_DIM:, :] = jnp.ones((16, tokens), jnp.bfloat16)
            return carry

        lax.fori_loop(0, spans, place, 0)

    scaled = query[0].astype(jnp.float32) * (math.log2(math.e) * HEAD_DIM**-0.5)
    turned = jnp.concatenate(
        [scaled[:, h * HEAD_DIM : (h + 1) * HEAD_DIM].T for h in range(heads)], axis=1
    )
    upper = turned.astype(jnp.bfloat16)
    lower = (turned - upper.astype(jnp.float32)).astype(jnp.bfloat16)
    weights = jnp.concatenate([upper, lower], axis=0)

    place = order[step * columns + ids[1]]
    tile = TILE_SPANS * tokens

    def attend(index, state, mask):
        best, summed = state
        block = keys[pl.ds(index * TILE_SPANS, TILE_SPANS)].reshape(tile, HEAD_DIM)
        scores = jnp.dot(
            jnp.concatenate([block, block], axis=1), weights, preferred_element_type=jnp.float32
        )
        if mask:
            row = lax.broadcasted_iota(jnp.int32, (tile, wide), 0) + index * tile
            col = lax.broadcasted_iota(jnp.int32, (tile, wide), 1) % tokens + place * tokens
            scores = jnp.where(row <= col, scores, masked_score)
        newest = jnp.maximum(best, jnp.max(scores, axis=0, keepdims=True))
        shrink = jnp.exp2(best - newest)
        raised = jnp.exp2(scores - newest).astype(jnp.bfloat16)
        block = values[pl.ds(index * TILE_SPANS, TILE_SPANS)]
        block = jnp.concatenate([block[i] for i in range(TILE_SPANS)], axis=1)
        update = jnp.dot(block, raised, preferred_element_type=jnp.float32)
        return newest, summed * shrink + update

    state = (
        jnp.full((1, wide), masked_score, jnp.float32),
        jnp.zeros((HEAD_DIM + 16, wide), jnp.float32),
    )
    whole = place // TILE_SPANS
    state = lax.fori_loop(0, whole, lambda i, s: attend(i, s, False), state)
    best, summed = attend(whole, state, True)
    result = summed[:HEAD_DIM] * (1.0 / summed[HEAD_DIM : HEAD_DIM + 1])
    for h in range(heads):
        out[0, :, h * HEAD_DIM : (h + 1) * HEAD_DIM] = (
            result[:, h * tokens : (h + 1) * tokens].T.astype(jnp.bfloat16)
        )


def shards(query, key, value, span_order):
    rows = lax.axis_size("row")
    columns = lax.axis_size("col")
    row_id = lax.axis_index("row")
    col_id = lax.axis_index("col")
    tokens = key.shape[0]
    spans = rows * columns
    half = tokens // 2
    heads = QHEADS // rows
    sharing = rows // KVHEADS
    width = heads * HEAD_DIM

    pair = jnp.stack([key, value]).reshape(2, 2, half, KVHEADS, HEAD_DIM)
    pair = pair.transpose(3, 1, 0, 2, 4)
    pair = jnp.broadcast_to(
        pair[:, None, :, None], (KVHEADS, sharing // 2, 2, columns, 2, half, HEAD_DIM)
    ).reshape(spans, 2, half, HEAD_DIM)
    mine = lax.all_to_all(pair, ("row", "col"), split_axis=0, concat_axis=0, tiled=True)
    other = lax.ppermute(mine, "row", [(i, i ^ 1) for i in range(rows)])

    ids = jnp.stack([row_id, col_id, row_id % 2]).astype(jnp.int32)
    full = lambda shape: pl.BlockSpec(shape, lambda s, order, ids: (0,) * len(shape))
    result = pl.pallas_call(
        functools.partial(attention_kernel, spans=spans, columns=columns, tokens=tokens),
        grid_spec=pltpu.PrefetchScalarGridSpec(
            num_scalar_prefetch=2,
            grid=(rows,),
            in_specs=[
                pl.BlockSpec((1, tokens, width), lambda s, order, ids: (s, 0, ids[0])),
                full(mine.shape),
                full(other.shape),
            ],
            out_specs=pl.BlockSpec((1, tokens, width), lambda s, order, ids: (s, 0, 0)),
            scratch_shapes=[
                pltpu.VMEM((spans, tokens, HEAD_DIM), jnp.bfloat16),
                pltpu.VMEM((spans, HEAD_DIM + 16, tokens), jnp.bfloat16),
            ],
        ),
        out_shape=jax.ShapeDtypeStruct((rows, tokens, width), jnp.bfloat16),
        compiler_params=pltpu.CompilerParams(vmem_limit_bytes=56 * 2**20),
        name="attention",
    )(span_order, ids, query, mine, other)
    result = lax.all_to_all(result, "row", split_axis=0, concat_axis=0, tiled=True)
    return result.transpose(1, 0, 2).reshape(tokens, rows * width)


def solution(mesh):
    placed = (P(None, "col", None), P(("row", "col"), None), P(("row", "col"), None), P())
    return jax.shard_map(
        shards, mesh=mesh, in_specs=placed, out_specs=P(("row", "col"), None), check_vma=False
    )
```

time: 372 us -> 95.8 us (0.26)
  waiting for transfers between devices: 120 us -> 1.73 us
  matrix products: 68.2 us -> 0 us
  other arithmetic: 49 us -> 0.74 us
  Pallas kernels: 0 us -> 33.9 us
  local copies, waits for them, and re-layouts: 36.6 us -> 5.11 us
  starting transfers between devices: 23.6 us -> 1.65 us
  blocking collectives: 69 us -> 50.9 us
    ppermute x12 -> x1, waiting for transfers between devices: 71.3 us -> 1.73 us  [shards(): other = lax.ppermute(mine, 'row', [(i, i ^ 1) for i in range(rows)])]
    dot_general x64 -> x0, matrix products: 68.2 us -> none  [the longest x32 48.9 us: attend(): jnp.einsum('nkgd,skd->nkgs', queries, keys, preferred_element_type=jnp.fl...]
    all_to_all x5 -> x0, waiting for transfers between devices: 49.1 us -> none  [the longest x2 49.1 us: shards(): lax.all_to_all(partial_value.reshape(rows, block_rows, group * HEAD_DIM),...]
    pallas_call x0 -> x1, Pallas kernels: none -> 33.9 us  [shards(): pl.pallas_call(functools.partial(attention_kernel, spans=spans, columns=c...]
    reduce_sum x42 -> x0, other arithmetic: 28.1 us -> none  [the longest x32 21.5 us: attend(): total = jnp.sum(raised, axis=-1)]
    all_to_all x5 -> x0, starting transfers between devices: 20.3 us -> none  [the longest x3 11.6 us: shards(): lax.all_to_all(log_sum.reshape(rows, block_rows, group), 'row', split_axi...]
    all_to_all x3 -> x2, blocking collectives: 69 us -> 50.9 us  [the longest x1 32.1 us: shards(): lax.all_to_all(pair, ('row', 'col'), split_axis=0, concat_axis=0, tiled=T...]
    unnamed x16 -> x4, local copies, waits for them, and re-layouts: 15.7 us -> 0.98 us
  transfers between devices with their start and end apart: 17 -> 1, of which waited for: 14 -> 1; matrix products, arithmetic and copies ran while one was open for 29% -> 1% of each run, Pallas kernels for 0% -> 0%
where the time goes in v1:
time: 95.8 us; the launch traced here: 94 us
  blocking collectives  50.9 us (53%)
  Pallas kernels  33.9 us (35%)
  local copies, waits for them, and re-layouts  5.11 us (5%)
  waiting for transfers between devices  1.73 us (2%)
  starting transfers between devices  1.65 us (2%)
    pallas_call x1, Pallas kernels, shards(): pl.pallas_call(functools.partial(attention_kernel, spans=spans, columns=c...  33.9 us
    all_to_all x1, blocking collectives, shards(): lax.all_to_all(pair, ('row', 'col'), split_axis=0, concat_axis=0, tiled=T...  32.1 us
    all_to_all x1, blocking collectives, shards(): lax.all_to_all(result, 'row', split_axis=0, concat_axis=0, tiled=True)  18.8 us
  transfers between devices with their start and end apart: 1, of which 1 were waited for; matrix products, arithmetic and copies ran while one was open for 1% of the time, Pallas kernels for 0%

profile of v1, /device:TPU:0, one launch (start us, length us, event | category | flops | bytes accessed | tf_op | source)
XLA Modules:
  0.0 94.0 jit_solution(15471525925887243025)
XLA Ops:
  0.0 0.9 stack.25
  0.9 0.9 %stack.26 = bf16[1,2,64,4,128]{4,3,2,1,0:T(4,128)(2,1)S(1)} reshape(bf16[128,512]{1,0:T(8,128)(2,1)} %param.6) | data formatting | bytes 262144 | tf_op jit(solution)/shard_map/stack | solution.py:99
  1.9 0.2 maximum_bitcast_fusion
  2.1 0.2 broadcast_in_dim.2
  2.4 32.1 %all_to_all.10.mine = bf16[32,2,64,128]{3,2,1,0:T(8,128)(2,1)S(1)} all-to-all(bf16[32,2,64,128]{3,2,1,0:T(8,128)(2,1)S(1)} %bitcast.8), channel_id=1, replica_groups=mesh['row'=8,'col'=4] {'row','col'}, dimensions={0} | all-to-all | bytes 2097152 | tf_op jit(solution)/shard_map/all_to_all | solution.py:104
  34.4 0.0 copy-start
  34.4 1.7 %collective-permute-start = (bf16[32,2,64,128]{3,2,1,0:T(8,128)(2,1)S(1)}, bf16[32,2,64,128]{3,2,1,0:T(8,128)(2,1)S(1)}, u32[]{:S(2)}, u32[]{:S(2)}) collective-permute-start(bf16[32,2,64,128]{3,2,1,0:T(8,128)(2,1)S(1)} %all_to_all.10.mine), channel_id=1, source_target_pairs={{0,4},{4,0},{8,12},{12,8},{16,20},{20,16},{24,28},{28,24},{1,5},{5... | collective-permute-start | bytes 3145736 | tf_op jit(solution)/shard_map/ppermute | solution.py:105
  36.1 0.6 pad_add_fusion.ids
  36.7 1.7 %collective-permute-done.other = bf16[32,2,64,128]{3,2,1,0:T(8,128)(2,1)S(1)} collective-permute-done((bf16[32,2,64,128]{3,2,1,0:T(8,128)(2,1)S(1)}, bf16[32,2,64,128]{3,2,1,0:T(8,128)(2,1)S(1)}, u32[]{:S(2)}, u32[]{:S(2)}) %collective-permute-start) | collective-permute-done | bytes 1048608 | tf_op jit(solution)/shard_map/ppermute | solution.py:105
  38.4 0.0 copy-done
  38.4 0.0 copy-start.1
  38.4 1.0 %copy-done.1 = bf16[32,2,64,128]{3,2,1,0:T(8,128)(2,1)} copy-done((bf16[32,2,64,128]{3,2,1,0:T(8,128)(2,1)}, bf16[32,2,64,128]{3,2,1,0:T(8,128)(2,1)S(1)}, u32[]{:S(2)}) %copy-start.1) | copy-done | bytes 1048600
  39.4 33.9 %attention.1 = bf16[8,128,512]{2,1,0:T(8,128)(2,1)} custom-call(s32[32]{0:T(128)} %order.1, s32[3]{0:T(128)} %pad_add_fusion.ids, bf16[8,128,4096]{2,1,0:T(8,128)(2,1)} %query.1, bf16[32,2,64,128]{3,2,1,0:T(8,128)(2,1)} %copy-done, bf16[32,2,64,128]{3,2,1,0:T(8,128)(2,1)} %copy-done.1), custom_call_target="tpu_custom_call" | custom-call | tf_op jit(solution)/shard_map/attention/pallas_call | solution.py:109
  73.3 18.8 %all_to_all.11 = bf16[8,128,512]{2,1,0:T(8,128)(2,1)S(1)} all-to-all(bf16[8,128,512]{2,1,0:T(8,128)(2,1)} %attention.1), channel_id=1, replica_groups=mesh['row'=8,'col'=4] {'row'}, dimensions={0} | all-to-all | bytes 2097152 | tf_op jit(solution)/shard_map/all_to_all | solution.py:129
  92.1 0.7 copy.7
  92.7 1.3 %copy.8 = bf16[128,4096]{1,0:T(8,128)(2,1)} copy(bf16[128,4096]{0,1:T(8,128)(2,1)S(1)} %bitcast.10) | data formatting | bytes 2097152 | tf_op jit(solution)/shard_map/reshape | solution.py:130
  (1 shorter events, 0.0 us)
Async XLA Ops:
  34.4 3.9 %copy-start = (bf16[32,2,64,128]{3,2,1,0:T(8,128)(2,1)}, bf16[32,2,64,128]{3,2,1,0:T(8,128)(2,1)S(1)}, u32[]{:S(2)}) copy-start(bf16[32,2,64,128]{3,2,1,0:T(8,128)(2,1)S(1)} %all_to_all.10.mine) | copy-start | bytes 3145732
  34.4 3.9 %collective-permute-start = (bf16[32,2,64,128]{3,2,1,0:T(8,128)(2,1)S(1)}, bf16[32,2,64,128]{3,2,1,0:T(8,128)(2,1)S(1)}, u32[]{:S(2)}, u32[]{:S(2)}) collective-permute-start(bf16[32,2,64,128]{3,2,1,0:T(8,128)(2,1)S(1)} %all_to_all.10.mine), channel_id=1, source_target_pairs={{0,4},{4,0},{8,12},{12,8},{16,20},{20,16},{24,28},{28,24},{1,5},{5... | collective-permute-start | bytes 3145736 | tf_op jit(solution)/shard_map/ppermute | solution.py:105
  38.4 1.0 %copy-start.1 = (bf16[32,2,64,128]{3,2,1,0:T(8,128)(2,1)}, bf16[32,2,64,128]{3,2,1,0:T(8,128)(2,1)S(1)}, u32[]{:S(2)}) copy-start(bf16[32,2,64,128]{3,2,1,0:T(8,128)(2,1)S(1)} %collective-permute-done.other) | copy-start | bytes 3145732

commit v2 on v1

v2 whole, which is shorter than its diff:
```python
import functools
import math

import jax
import jax.numpy as jnp
from jax import lax
from jax.experimental import pallas as pl
from jax.experimental.pallas import tpu as pltpu
from jax.sharding import PartitionSpec as P


HEAD_DIM = 128
QHEADS = 32
KVHEADS = 4
TILE_SPANS = 2
EXTRA = 16

masked_score = -1e30


def attention_kernel(*refs, pieces, first, last, tokens):
    refs = list(refs)
    meta = refs.pop(0)
    blocks = [refs.pop(0) for _ in range(pieces)]
    if first:
        query = refs.pop(0)
    else:
        qt_in, best_in, acc_in = (refs.pop(0) for _ in range(3))
    if last:
        out = refs.pop(0)
    else:
        qt_out, best_out, acc_out = (refs.pop(0) for _ in range(3))
    keys, values, best, acc, s0, s1, p0, p1, items = refs[:9]
    qt = qt_out if first and not last else (refs[9] if first else qt_in)
    steps, _, wide = qt.shape
    heads = wide // HEAD_DIM
    spans = sum(block.shape[0] for block in blocks)
    per = blocks[0].shape[0]
    tile = TILE_SPANS * tokens

    for index, block in enumerate(blocks):
        def place(span, carry, block=block, index=index):
            spot = meta[index * per + span]
            keys[spot] = block[span, 0]
            values[spot, :HEAD_DIM] = block[span, 1].astype(jnp.float32).T.astype(jnp.bfloat16)
            values[spot, HEAD_DIM:] = jnp.ones((EXTRA, tokens), jnp.bfloat16)
            return carry

        lax.fori_loop(0, per, place, 0, unroll=4)

    def count(s):
        return meta[spans + s]

    if first:
        def turn(s, carry):
            scaled = query[s].astype(jnp.float32) * (math.log2(math.e) * HEAD_DIM**-0.5)
            for h in range(heads):
                lanes = slice(h * HEAD_DIM, (h + 1) * HEAD_DIM)
                turned = scaled[:, lanes].T
                upper = turned.astype(jnp.bfloat16)
                qt[s, :HEAD_DIM, lanes] = upper
                qt[s, HEAD_DIM:, lanes] = (turned - upper.astype(jnp.float32)).astype(jnp.bfloat16)
            return carry

        lax.fori_loop(0, steps, turn, 0, unroll=2)

        row = lax.broadcasted_iota(jnp.int32, (tokens, wide), 0)
        col = lax.broadcasted_iota(jnp.int32, (tokens, wide), 1) % tokens
        seen = row <= col

        def diagonal(pair, carry):
            for s in (pair * 2, pair * 2 + 1):
                spot = count(s)
                block = keys[spot]
                scores = jnp.dot(
                    jnp.concatenate([block, block], axis=1), qt[s], preferred_element_type=jnp.float32
                )
                scores = jnp.where(seen, scores, masked_score)
                top = jnp.max(scores, axis=0, keepdims=True)
                raised = jnp.exp2(scores - top).astype(jnp.bfloat16)
                best[s] = top
                acc[s] = jnp.dot(values[spot], raised, preferred_element_type=jnp.float32)
            return carry

        lax.fori_loop(0, steps // 2, diagonal, 0)
    else:
        def load(s, carry):
            best[s] = best_in[s]
            acc[s] = acc_in[s]
            return carry

        lax.fori_loop(0, steps, load, 0)
    best[steps] = jnp.zeros((1, wide), jnp.float32)
    acc[steps] = jnp.zeros(acc.shape[1:], jnp.float32)
    p1[...] = jnp.zeros(p1.shape, p1.dtype)

    idle = steps * 256
    items[0] = idle

    def list_span(s, n):
        def one(t, n):
            items[n] = s * 256 + t
            return n + 1

        return lax.fori_loop(0, lax.div(count(s) + (TILE_SPANS - 1), jnp.int32(TILE_SPANS)), one, n)

    n = lax.fori_loop(0, steps, list_span, 1)
    for k in range(4):
        items[n + k] = idle

    def split(i):
        item = items[i]
        return item >> 8, item & 255

    def score(i, target):
        s, t = split(i)
        block = keys[pl.ds(t * TILE_SPANS, TILE_SPANS)].reshape(tile, HEAD_DIM)
        scores = jnp.dot(
            jnp.concatenate([block, block], axis=1),
            qt[jnp.minimum(s, steps - 1)],
            preferred_element_type=jnp.float32,
        )
        target[...] = scores
        return [
            jnp.max(scores[j * tokens : (j + 1) * tokens], axis=0, keepdims=True)
            for j in range(TILE_SPANS)
        ]

    def soften(i, tops, source, target):
        s, t = split(i)
        left = jnp.where(s < steps, count(jnp.minimum(s, steps - 1)), 0) - t * TILE_SPANS
        old = best[s]
        new = old
        for j in range(TILE_SPANS):
            new = jnp.maximum(new, jnp.where(j < left, tops[j], masked_score))
        best[s] = new
        for j in range(TILE_SPANS):
            rows = slice(j * tokens, (j + 1) * tokens)
            base = jnp.where(j < left, new, -masked_score)
            target[rows] = jnp.exp2(source[rows] - base).astype(jnp.bfloat16)
        return jnp.exp2(old - new)

    def gather(i, shrink, source):
        s, t = split(i)
        block = values[pl.ds(t * TILE_SPANS, TILE_SPANS)]
        block = jnp.concatenate([block[j] for j in range(TILE_SPANS)], axis=1)
        acc[s] = acc[s] * shrink + jnp.dot(block, source[...], preferred_element_type=jnp.float32)

    def body(k, carry):
        tops, shrink = carry
        i = 1 + 2 * k
        tops_b = score(i + 1, s1)
        shrink_b = soften(i, tops, s0, p0)
        gather(i - 1, shrink, p1)
        tops_c = score(i + 2, s0)
        shrink_c = soften(i + 1, tops_b, s1, p1)
        gather(i, shrink_b, p0)
        return tops_c, shrink_c

    lax.fori_loop(0, (n + 1) >> 1, body, (score(1, s0), jnp.ones((1, wide), jnp.float32)))

    def finish(s, carry):
        if last:
            total = acc[s]
            result = total[:HEAD_DIM] * (1.0 / total[HEAD_DIM : HEAD_DIM + 1])
            for h in range(heads):
                lanes = slice(h * HEAD_DIM, (h + 1) * HEAD_DIM)
                out[s, :, lanes] = result[:, h * tokens : (h + 1) * tokens].T.astype(jnp.bfloat16)
        else:
            best_out[s] = best[s]
            acc_out[s] = acc[s]
            if not first:
                qt_out[s] = qt_in[s]
        return carry

    lax.fori_loop(0, steps, finish, 0, unroll=2)


def attend(meta, blocks, query, state, last, steps, tokens, width):
    first = query is not None
    spans = sum(block.shape[0] for block in blocks)
    room = -(-spans // TILE_SPANS) * TILE_SPANS
    tile = TILE_SPANS * tokens
    vmem = pl.BlockSpec(memory_space=pltpu.VMEM)
    operands = [*blocks, query] if first else [*blocks, *state]
    if last:
        shapes = [jax.ShapeDtypeStruct((steps, tokens, width), jnp.bfloat16)]
    else:
        shapes = [
            jax.ShapeDtypeStruct((steps, 2 * HEAD_DIM, width), jnp.bfloat16),
            jax.ShapeDtypeStruct((steps, 1, width), jnp.float32),
            jax.ShapeDtypeStruct((steps, HEAD_DIM + EXTRA, width), jnp.float32),
        ]
    scratch = [
        pltpu.VMEM((room, tokens, HEAD_DIM), jnp.bfloat16),
        pltpu.VMEM((room, HEAD_DIM + EXTRA, tokens), jnp.bfloat16),
        pltpu.VMEM((steps + 1, 1, width), jnp.float32),
        pltpu.VMEM((steps + 1, HEAD_DIM + EXTRA, width), jnp.float32),
        pltpu.VMEM((tile, width), jnp.float32),
        pltpu.VMEM((tile, width), jnp.float32),
        pltpu.VMEM((tile, width), jnp.bfloat16),
        pltpu.VMEM((tile, width), jnp.bfloat16),
        pltpu.SMEM((steps * (room // TILE_SPANS) + 8,), jnp.int32),
    ]
    if first and last:
        scratch.append(pltpu.VMEM((steps, 2 * HEAD_DIM, width), jnp.bfloat16))
    work = steps * spans * tokens * tokens * width * 2
    return pl.pallas_call(
        functools.partial(
            attention_kernel, pieces=len(blocks), first=first, last=last, tokens=tokens
        ),
        in_specs=[pl.BlockSpec(memory_space=pltpu.SMEM)] + [vmem] * len(operands),
        out_specs=[vmem] * len(shapes),
        out_shape=shapes,
        scratch_shapes=scratch,
        cost_estimate=pl.CostEstimate(
            flops=work, bytes_accessed=8 * 2**20, transcendentals=work // (4 * HEAD_DIM)
        ),
        compiler_params=pltpu.CompilerParams(vmem_limit_bytes=40 * 2**20),
        name="attention",
    )(meta, *operands)


def lookup(table, indices):
    columns = jnp.arange(table.shape[0], dtype=jnp.int32)
    chosen = jnp.where(indices[:, None] == columns[None, :], table[None, :], 0)
    return jnp.sum(chosen, axis=1)


def shards(query, key, value, span_order):
    rows = lax.axis_size("row")
    columns = lax.axis_size("col")
    row_id = lax.axis_index("row")
    col_id = lax.axis_index("col")
    tokens = key.shape[0]
    heads = QHEADS // rows
    sharing = rows // KVHEADS
    width = heads * HEAD_DIM
    deltas = list(range(0, rows, 2))

    def piece(row):
        start = lax.div(row, jnp.int32(sharing)) * HEAD_DIM
        return jnp.stack([lax.dynamic_slice_in_dim(x, start, HEAD_DIM, 1) for x in (key, value)])

    parts = [piece(row_id)]
    for delta in deltas[1:]:
        pairs = [(i, i ^ delta) for i in range(rows)]
        parts.append(lax.ppermute(piece(row_id ^ delta), "row", pairs))
    own = jnp.stack(parts)

    across = [(i, i ^ 1) for i in range(rows)]
    mine = [own]
    for s in range(1, columns):
        pairs = [(i, (i + s) % columns) for i in range(columns)]
        mine.append(lax.ppermute(own, "col", pairs))
    query_orders = lookup(span_order, jnp.arange(rows, dtype=jnp.int32) * columns + col_id)
    near = row_id ^ jnp.array(deltas, jnp.int32)
    taken = lax.dynamic_slice_in_dim(query, row_id * width, width, 2)

    def describe(shift):
        source = lax.rem(col_id + (columns - shift), jnp.int32(columns))
        held = jnp.concatenate([near, near ^ 1]) * columns + source
        orders = lookup(span_order, held)
        rank = jnp.sum(orders[None, :] < orders[:, None], axis=1)
        count = jnp.sum(orders[None, :] < query_orders[:, None], axis=1)
        return jnp.concatenate([rank, count]).astype(jnp.int32)

    state = None
    for shift, block in enumerate(mine):
        if state is not None:
            block, tops = lax.optimization_barrier((block, state[1]))
            state = [state[0], tops, state[2]]
        meta = describe(shift)
        other = lax.ppermute(block, "row", across)
        state = attend(
            meta,
            [block, other],
            taken if shift == 0 else None,
            state,
            shift == columns - 1,
            rows,
            tokens,
            width,
        )
    result = lax.all_to_all(state[0], "row", split_axis=0, concat_axis=0, tiled=True)
    return result.transpose(1, 0, 2).reshape(tokens, rows * width)


def solution(mesh):
    placed = (P(None, "col", None), P(("row", "col"), None), P(("row", "col"), None), P())

    return jax.shard_map(
        shards, mesh=mesh, in_specs=placed, out_specs=P(("row", "col"), None), check_vma=False
    )
```

time: 95.8 us -> 76 us (0.79); the launches traced: 94 us -> 75.7 us
  blocking collectives: 50.9 us -> 17.8 us
  waiting for transfers between devices: 1.73 us -> 12.6 us
  starting transfers between devices: 1.65 us -> 11.5 us
  Pallas kernels: 33.9 us -> 28 us
  local copies, waits for them, and re-layouts: 5.11 us -> 4.15 us
    all_to_all x2 -> x1, blocking collectives: 50.9 us -> 17.8 us  [shards(): lax.all_to_all(state[0], 'row', split_axis=0, concat_axis=0, tiled=True)]
    ppermute x1 -> x10, waiting for transfers between devices: 1.73 us -> 12.6 us  [the longest x3 6.99 us: shards(): mine.append(lax.ppermute(own, 'col', pairs))]
    ppermute x1 -> x10, starting transfers between devices: 1.65 us -> 11.5 us  [the longest x3 6.46 us: shards(): mine.append(lax.ppermute(own, 'col', pairs))]
    pallas_call x1 -> x4, Pallas kernels: 33.9 us -> 28 us  [attend(): pl.pallas_call(functools.partial(attention_kernel, pieces=len(blocks), fi...]
    dynamic_slice x0 -> x1, local copies, waits for them, and re-layouts: none -> 1.29 us  [shards(): taken = lax.dynamic_slice_in_dim(query, row_id * width, width, 2)]
    reduce_sum x0 -> x2, other arithmetic: none -> 1.2 us  [the longest x1 0.91 us: lookup(): return jnp.sum(chosen, axis=1)]
    another operation x2 -> x1, local copies, waits for them, and re-layouts: 1.88 us -> 0.89 us  [piece(): jnp.stack([lax.dynamic_slice_in_dim(x, start, HEAD_DIM, 1) for x in (key,...]
    unnamed x4 -> x0, local copies, waits for them, and re-layouts: 0.98 us -> none
  transfers between devices with their start and end apart: 1 -> 10, of which waited for: 1 -> 5; matrix products, arithmetic and copies ran while one was open for 1% -> 4% of each run, Pallas kernels for 0% -> 27%
where the time goes in v2:
time: 76 us; the launch traced here: 75.7 us
  Pallas kernels  28 us (37%)
  blocking collectives  17.8 us (23%)
  waiting for transfers between devices  12.6 us (17%)
  starting transfers between devices  11.5 us (15%)
  local copies, waits for them, and re-layouts  4.15 us (5%)
  other arithmetic  1.66 us (2%)
    pallas_call x4, Pallas kernels, attend(): pl.pallas_call(functools.partial(attention_kernel, pieces=len(blocks), fi...  28 us
    all_to_all x1, blocking collectives, shards(): lax.all_to_all(state[0], 'row', split_axis=0, concat_axis=0, tiled=True)  17.8 us
    ppermute x3, waiting for transfers between devices, shards(): mine.append(lax.ppermute(own, 'col', pairs))  6.99 us
    ppermute x3, starting transfers between devices, shards(): mine.append(lax.ppermute(own, 'col', pairs))  6.46 us
    ppermute x3, starting transfers between devices, shards(): parts.append(lax.ppermute(piece(row_id ^ delta), 'row', pairs))  4.68 us
    ppermute x3, waiting for transfers between devices, shards(): parts.append(lax.ppermute(piece(row_id ^ delta), 'row', pairs))  4.1 us
  transfers between devices with their start and end apart: 10, of which 5 were waited for; matrix products, arithmetic and copies ran while one was open for 4% of the time, Pallas kernels for 27%

profile of v2, /device:TPU:0, one launch (start us, length us, event | category | flops | bytes accessed | tf_op | source)
XLA Modules:
  0.0 75.7 jit_solution(9725523696305052198)
XLA Ops:
  0.0 0.9 %dynamic-slice_bitcast_fusion.6 = (bf16[1,128,128]{2,1,0:T(8,128)(2,1)S(1)}, bf16[1,128,128]{2,1,0:T(8,128)(2,1)S(1)}, bf16[1,128,128]{2,1,0:T(8,128)(2,1)S(1)},...) fusion(bf16[128,512]{1,0:T(8,128)(2,1)} %param.7, ...), kind=kLoop, calls=%fused_computation.11 | loop fusion | bytes 524304 | tf_op jit(solution)/shard_map/stack | solution.py:243
  0.9 3.0 %collective-permute-start = (bf16[2,128,128]{2,1,0:T(8,128)(2,1)S(1)}, bf16[2,128,128]{2,1,0:T(8,128)(2,1)S(1)}, u32[]{:S(2)}, u32[]{:S(2)}) collective-permute-start(bf16[2,128,128]{2,1,0:T(8,128)(2,1)S(1)} %pad_maximum_fusion.1), channel_id=1, source_target_pairs={{0,8},{4,12},{8,0},{12,4},{16,24},{20,28},{24,16},{28,20},{1,9},{5... | collective-permute-start | bytes 196616 | tf_op jit(solution)/shard_map/ppermute | solution.py:248
  4.0 1.6 %collective-permute-start.1 = (bf16[2,128,128]{2,1,0:T(8,128)(2,1)S(1)}, bf16[2,128,128]{2,1,0:T(8,128)(2,1)S(1)}, u32[]{:S(2)}, u32[]{:S(2)}) collective-permute-start(bf16[2,128,128]{2,1,0:T(8,128)(2,1)S(1)} %pad_maximum_fusion.2), channel_id=1, source_target_pairs={{0,16},{4,20},{8,24},{12,28},{16,0},{20,4},{24,8},{28,12},{1,17},{... | collective-permute-start | bytes 196616 | tf_op jit(solution)/shard_map/ppermute | solution.py:248
  5.7 0.1 broadcast_add_fusion.3
  5.7 0.9 %select_reduce_fusion = (s32[8]{0:T(128)S(1)}, s32[8]{0:T(128)S(1)}, s32[8]{0:T(128)S(1)}, s32[8]{0:T(128)S(1)}, s32[8]{0:T(128)S(1)}) fusion(s32[8]{0:T(128)S(1)} %get-tuple-element.60, s32[32]{0:T(128)} %param.8, s32[8]{0:T(128)S(1)} %multiply_add_fusion, s32[8]{0:T(128)S(1)} %get-tuple-element.59, s32[8]{0:T(128)S(1)} %get-tuple-element.58, ...), kind=kLoop, calls=%fused_computation.15 | loop fusion | flops 3800 | bytes 448 | tf_op jit(solution)/shard_map/reduce_sum | solution.py:227
  6.7 1.6 %collective-permute-done.1 = bf16[2,128,128]{2,1,0:T(8,128)(2,1)S(1)} collective-permute-done((bf16[2,128,128]{2,1,0:T(8,128)(2,1)S(1)}, bf16[2,128,128]{2,1,0:T(8,128)(2,1)S(1)}, u32[]{:S(2)}, u32[]{:S(2)}) %collective-permute-start.1) | collective-permute-done | bytes 65568 | tf_op jit(solution)/shard_map/ppermute | solution.py:248
  8.3 2.5 %collective-permute-done.2 = bf16[2,128,128]{2,1,0:T(8,128)(2,1)S(1)} collective-permute-done((bf16[2,128,128]{2,1,0:T(8,128)(2,1)S(1)}, bf16[2,128,128]{2,1,0:T(8,128)(2,1)S(1)}, u32[]{:S(2)}, u32[]{:S(2)}) %collective-permute-start.2) | collective-permute-done | bytes 65568 | tf_op jit(solution)/shard_map/ppermute | solution.py:248
  10.9 0.3 convert_reduce_fusion.1
  11.2 1.6 %collective-permute-start.5 = (bf16[4,2,128,128]{3,2,1,0:T(8,128)(2,1)S(1)}, bf16[4,2,128,128]{3,2,1,0:T(8,128)(2,1)S(1)}, u32[]{:S(2)}, u32[]{:S(2)}) collective-permute-start(bf16[4,2,128,128]{3,2,1,0:T(8,128)(2,1)S(1)} %pad_maximum_fusion.refs_1_), channel_id=1, source_target_pairs={{0,1},{1,2},{2,3},{3,0},{4,5},{5,6},{6,7},{7,4},{8,9},{9,10},{10,1... | collective-permute-start | bytes 786440 | tf_op jit(solution)/shard_map/ppermute | solution.py:255
  12.8 0.1 pad_add_fusion.3.refs_0_
  12.9 1.3 %constant_dynamic-slice_fusion.refs_3_ = bf16[8,128,512]{2,1,0:T(8,128)(2,1)S(1)} fusion(bf16[8,128,4096]{2,1,0:T(8,128)(2,1)} %param.5, s32[]{:T(128)S(6)} %select_n.44), kind=kLoop, calls=%fused_computation.31 | loop fusion | bytes 2097156 | tf_op jit(solution)/shard_map/dynamic_slice | solution.py:258
  14.2 8.6 %attention.4 = (bf16[8,256,512]{2,1,0:T(8,128)(2,1)S(1)}, f32[8,1,512]{2,1,0:T(1,128)S(1)}, f32[8,144,512]{2,1,0:T(8,128)S(1)}) custom-call(s32[16]{0:T(128)S(1)} %pad_add_fusion.3.refs_0_, bf16[4,2,128,128]{3,2,1,0:T(8,128)(2,1)S(1)} %pad_maximum_fusion.refs_1_, bf16[4,2,128,128]{3,2,1,0:T(8,128)(2,1)S(1)} %collective-permute-done.6.refs_2_, ...), custom_call_target="tpu_custom_call" | custom-call | flops 1073741824 | bytes 8388608 | tf_op jit(solution)/shard_map/attention/pallas_call | solution.py:208
  22.8 0.3 collective-permute-start.7
  23.1 2.6 %collective-permute-start.4 = (bf16[4,2,128,128]{3,2,1,0:T(8,128)(2,1)S(1)}, bf16[4,2,128,128]{3,2,1,0:T(8,128)(2,1)S(1)}, u32[]{:S(2)}, u32[]{:S(2)}) collective-permute-start(bf16[4,2,128,128]{3,2,1,0:T(8,128)(2,1)S(1)} %pad_maximum_fusion.refs_1_), channel_id=1, source_target_pairs={{0,2},{1,3},{2,0},{3,1},{4,6},{5,7},{6,4},{7,5},{8,10},{9,11},{10,... | collective-permute-start | bytes 786440 | tf_op jit(solution)/shard_map/ppermute | solution.py:255
  25.8 6.5 %attention.5 = (bf16[8,256,512]{2,1,0:T(8,128)(2,1)S(1)}, f32[8,1,512]{2,1,0:T(1,128)S(1)}, f32[8,144,512]{2,1,0:T(8,128)S(1)}) custom-call(s32[16]{0:T(128)S(1)} %pad_add_fusion.2.refs_0_, bf16[4,2,128,128]{3,2,1,0:T(8,128)(2,1)S(1)} %collective-permute-done.5.refs_1_, bf16[4,2,128,128]{3,2,1,0:T(8,128)(2,1)S(1)} %collective-permute-done.7.refs_2_, ...), custom_call_target="tpu_custom_call" | custom-call | flops 1073741824 | bytes 8388608 | tf_op jit(solution)/shard_map/attention/pallas_call | solution.py:208
  32.3 5.8 %collective-permute-done.4.refs_1_ = bf16[4,2,128,128]{3,2,1,0:T(8,128)(2,1)S(1)} collective-permute-done((bf16[4,2,128,128]{3,2,1,0:T(8,128)(2,1)S(1)}, bf16[4,2,128,128]{3,2,1,0:T(8,128)(2,1)S(1)}, u32[]{:S(2)}, u32[]{:S(2)}) %collective-permute-start.4) | collective-permute-done | bytes 262176 | tf_op jit(solution)/shard_map/ppermute | solution.py:255
  38.1 2.2 %collective-permute-start.3 = (bf16[4,2,128,128]{3,2,1,0:T(8,128)(2,1)S(1)}, bf16[4,2,128,128]{3,2,1,0:T(8,128)(2,1)S(1)}, u32[]{:S(2)}, u32[]{:S(2)}) collective-permute-start(bf16[4,2,128,128]{3,2,1,0:T(8,128)(2,1)S(1)} %pad_maximum_fusion.refs_1_), channel_id=1, source_target_pairs={{0,3},{1,0},{2,1},{3,2},{4,7},{5,4},{6,5},{7,6},{8,11},{9,8},{10,9... | collective-permute-start | bytes 786440 | tf_op jit(solution)/shard_map/ppermute | solution.py:255
  40.4 5.3 %attention.6 = (bf16[8,256,512]{2,1,0:T(8,128)(2,1)S(1)}, f32[8,1,512]{2,1,0:T(1,128)S(1)}, f32[8,144,512]{2,1,0:T(8,128)S(1)}) custom-call(s32[16]{0:T(128)S(1)} %pad_add_fusion.1.refs_0_, bf16[4,2,128,128]{3,2,1,0:T(8,128)(2,1)S(1)} %collective-permute-done.4.refs_1_, bf16[4,2,128,128]{3,2,1,0:T(8,128)(2,1)S(1)} %collective-permute-done.8.refs_2_, ...), custom_call_target="tpu_custom_call" | custom-call | flops 1073741824 | bytes 8388608 | tf_op jit(solution)/shard_map/attention/pallas_call | solution.py:208
  45.7 1.2 %collective-permute-done.3.refs_1_ = bf16[4,2,128,128]{3,2,1,0:T(8,128)(2,1)S(1)} collective-permute-done((bf16[4,2,128,128]{3,2,1,0:T(8,128)(2,1)S(1)}, bf16[4,2,128,128]{3,2,1,0:T(8,128)(2,1)S(1)}, u32[]{:S(2)}, u32[]{:S(2)}) %collective-permute-start.3) | collective-permute-done | bytes 262176 | tf_op jit(solution)/shard_map/ppermute | solution.py:255
  46.9 1.5 %collective-permute-done.9.refs_2_ = bf16[4,2,128,128]{3,2,1,0:T(8,128)(2,1)S(1)} collective-permute-done((bf16[4,2,128,128]{3,2,1,0:T(8,128)(2,1)S(1)}, bf16[4,2,128,128]{3,2,1,0:T(8,128)(2,1)S(1)}, u32[]{:S(2)}, u32[]{:S(2)}) %collective-permute-start.9) | collective-permute-done | bytes 262176 | tf_op jit(solution)/shard_map/ppermute | solution.py:274
  48.4 7.6 %attention.7 = bf16[8,128,512]{2,1,0:T(8,128)(2,1)S(1)} custom-call(s32[16]{0:T(128)S(1)} %pad_add_fusion.refs_0_, bf16[4,2,128,128]{3,2,1,0:T(8,128)(2,1)S(1)} %collective-permute-done.3.refs_1_, bf16[4,2,128,128]{3,2,1,0:T(8,128)(2,1)S(1)} %collective-permute-done.9.refs_2_, bf16[8,256,512]{2,1,0:T(8,128)(2,1)S(1)} %get-tuple-element.32.refs_3_, ...), custom_call_target="tpu_custom_call" | custom-call | flops 1073741824 | bytes 8388608 | tf_op jit(solution)/shard_map/attention/pallas_call | solution.py:208
  56.0 17.8 %all_to_all.5 = bf16[8,128,512]{2,1,0:T(8,128)(2,1)S(1)} all-to-all(bf16[8,128,512]{2,1,0:T(8,128)(2,1)S(1)} %attention.7), channel_id=1, replica_groups=mesh['row'=8,'col'=4] {'row'}, dimensions={0} | all-to-all | bytes 2097152 | tf_op jit(solution)/shard_map/all_to_all | solution.py:285
  73.7 0.7 copy.8
  74.4 1.3 %copy.9 = bf16[128,4096]{1,0:T(8,128)(2,1)} copy(bf16[128,4096]{0,1:T(8,128)(2,1)S(1)} %bitcast.24) | data formatting | bytes 2097152 | tf_op jit(solution)/shard_map/reshape | solution.py:286
  (20 shorter events, 0.5 us)
Async XLA Ops:
  0.9 5.8 %collective-permute-start = (bf16[2,128,128]{2,1,0:T(8,128)(2,1)S(1)}, bf16[2,128,128]{2,1,0:T(8,128)(2,1)S(1)}, u32[]{:S(2)}, u32[]{:S(2)}) collective-permute-start(bf16[2,128,128]{2,1,0:T(8,128)(2,1)S(1)} %pad_maximum_fusion.1), channel_id=1, source_target_pairs={{0,8},{4,12},{8,0},{12,4},{16,24},{20,28},{24,16},{28,20},{1,9},{5... | collective-permute-start | bytes 196616 | tf_op jit(solution)/shard_map/ppermute | solution.py:248
  4.0 4.3 %collective-permute-start.1 = (bf16[2,128,128]{2,1,0:T(8,128)(2,1)S(1)}, bf16[2,128,128]{2,1,0:T(8,128)(2,1)S(1)}, u32[]{:S(2)}, u32[]{:S(2)}) collective-permute-start(bf16[2,128,128]{2,1,0:T(8,128)(2,1)S(1)} %pad_maximum_fusion.2), channel_id=1, source_target_pairs={{0,16},{4,20},{8,24},{12,28},{16,0},{20,4},{24,8},{28,12},{1,17},{... | collective-permute-start | bytes 196616 | tf_op jit(solution)/shard_map/ppermute | solution.py:248
  5.5 5.2 %collective-permute-start.2 = (bf16[2,128,128]{2,1,0:T(8,128)(2,1)S(1)}, bf16[2,128,128]{2,1,0:T(8,128)(2,1)S(1)}, u32[]{:S(2)}, u32[]{:S(2)}) collective-permute-start(bf16[2,128,128]{2,1,0:T(8,128)(2,1)S(1)} %pad_maximum_fusion.3), channel_id=1, source_target_pairs={{0,24},{4,28},{8,16},{12,20},{16,8},{20,12},{24,0},{28,4},{1,25},{... | collective-permute-start | bytes 196616 | tf_op jit(solution)/shard_map/ppermute | solution.py:248
  10.8 3.4 %collective-permute-start.6 = (bf16[4,2,128,128]{3,2,1,0:T(8,128)(2,1)S(1)}, bf16[4,2,128,128]{3,2,1,0:T(8,128)(2,1)S(1)}, u32[]{:S(2)}, u32[]{:S(2)}) collective-permute-start(bf16[4,2,128,128]{3,2,1,0:T(8,128)(2,1)S(1)} %pad_maximum_fusion.refs_1_), channel_id=1, source_target_pairs={{0,4},{4,0},{8,12},{12,8},{16,20},{20,16},{24,28},{28,24},{1,5},{5... | collective-permute-start | bytes 786440 | tf_op jit(solution)/shard_map/ppermute | solution.py:274
  11.2 11.6 %collective-permute-start.5 = (bf16[4,2,128,128]{3,2,1,0:T(8,128)(2,1)S(1)}, bf16[4,2,128,128]{3,2,1,0:T(8,128)(2,1)S(1)}, u32[]{:S(2)}, u32[]{:S(2)}) collective-permute-start(bf16[4,2,128,128]{3,2,1,0:T(8,128)(2,1)S(1)} %pad_maximum_fusion.refs_1_), channel_id=1, source_target_pairs={{0,1},{1,2},{2,3},{3,0},{4,5},{5,6},{6,7},{7,4},{8,9},{9,10},{10,1... | collective-permute-start | bytes 786440 | tf_op jit(solution)/shard_map/ppermute | solution.py:255
  22.8 3.0 %collective-permute-start.7 = (bf16[4,2,128,128]{3,2,1,0:T(8,128)(2,1)S(1)}, bf16[4,2,128,128]{3,2,1,0:T(8,128)(2,1)S(1)}, u32[]{:S(2)}, u32[]{:S(2)}) collective-permute-start(bf16[4,2,128,128]{3,2,1,0:T(8,128)(2,1)S(1)} %collective-permute-done.5.refs_1_), channel_id=1, source_target_pairs={{0,4},{4,0},{8,12},{12,8},{16,20},{20,16},{24,28},{28,24},{1,5},{5... | collective-permute-start | bytes 786440 | tf_op jit(solution)/shard_map/ppermute | solution.py:274
  23.1 15.0 %collective-permute-start.4 = (bf16[4,2,128,128]{3,2,1,0:T(8,128)(2,1)S(1)}, bf16[4,2,128,128]{3,2,1,0:T(8,128)(2,1)S(1)}, u32[]{:S(2)}, u32[]{:S(2)}) collective-permute-start(bf16[4,2,128,128]{3,2,1,0:T(8,128)(2,1)S(1)} %pad_maximum_fusion.refs_1_), channel_id=1, source_target_pairs={{0,2},{1,3},{2,0},{3,1},{4,6},{5,7},{6,4},{7,5},{8,10},{9,11},{10,... | collective-permute-start | bytes 786440 | tf_op jit(solution)/shard_map/ppermute | solution.py:255
  38.1 2.3 %collective-permute-start.8 = (bf16[4,2,128,128]{3,2,1,0:T(8,128)(2,1)S(1)}, bf16[4,2,128,128]{3,2,1,0:T(8,128)(2,1)S(1)}, u32[]{:S(2)}, u32[]{:S(2)}) collective-permute-start(bf16[4,2,128,128]{3,2,1,0:T(8,128)(2,1)S(1)} %collective-permute-done.4.refs_1_), channel_id=1, source_target_pairs={{0,4},{4,0},{8,12},{12,8},{16,20},{20,16},{24,28},{28,24},{1,5},{5... | collective-permute-start | bytes 786440 | tf_op jit(solution)/shard_map/ppermute | solution.py:274
  38.1 8.7 %collective-permute-start.3 = (bf16[4,2,128,128]{3,2,1,0:T(8,128)(2,1)S(1)}, bf16[4,2,128,128]{3,2,1,0:T(8,128)(2,1)S(1)}, u32[]{:S(2)}, u32[]{:S(2)}) collective-permute-start(bf16[4,2,128,128]{3,2,1,0:T(8,128)(2,1)S(1)} %pad_maximum_fusion.refs_1_), channel_id=1, source_target_pairs={{0,3},{1,0},{2,1},{3,2},{4,7},{5,4},{6,5},{7,6},{8,11},{9,8},{10,9... | collective-permute-start | bytes 786440 | tf_op jit(solution)/shard_map/ppermute | solution.py:255
  46.8 1.5 %collective-permute-start.9 = (bf16[4,2,128,128]{3,2,1,0:T(8,128)(2,1)S(1)}, bf16[4,2,128,128]{3,2,1,0:T(8,128)(2,1)S(1)}, u32[]{:S(2)}, u32[]{:S(2)}) collective-permute-start(bf16[4,2,128,128]{3,2,1,0:T(8,128)(2,1)S(1)} %collective-permute-done.3.refs_1_), channel_id=1, source_target_pairs={{0,4},{4,0},{8,12},{12,8},{16,20},{20,16},{24,28},{28,24},{1,5},{5... | collective-permute-start | bytes 786440 | tf_op jit(solution)/shard_map/ppermute | solution.py:274
